TPU v7x, 32 devices: a whole 2x2x4 slice. The times are simulated.
32 devices in a mesh: group: 2 (over y), plane: 4 (over z), planey: 2 (over x), ens: 2 (over core).
Axes of the slice: x: 2, y: 2, z: 4, core: 2. Of those that a mesh axis runs over, the one named last changes fastest.
Arguments:
- u_prior: float32 [8, 2, 10, 64, 256], P(('group', 'ens'), None, None, 'plane', 'planey'), parts along dimension 0, may hold values from -6 to 6
- friction_rows: int32 [8], P(('group', 'ens')), parts along dimension 0, may hold values from 0 to 15
- friction_table: float32 [32, 64, 256], P('group', 'plane', 'planey'), parts along dimension 0, may hold values from 0.3 to 3
- bed_fixed: int32 [64, 256], P('plane', 'planey'), may hold values from -536870912 to 536870911
- ice_mask: int32 [64, 256], P('plane', 'planey'), may hold values 0 or 1
Outputs:
- mean_velocity: float32 [4, 10, 64, 256], P('group', None, 'plane', 'planey'), parts along dimension 0
There are 2 independent parts, one for each index of `group`. A program takes and returns all parts, laid end to end along the dimension named above; an argument that names none is the same for every part. Nothing has to cross between parts.
Inputs may be any that keep to these rules, and one draw needn't show every extreme that they name: `friction_rows`: each sample names one row of the friction table.
All inputs are finite; a program needn't handle non-finite values. No bound on the sum of `ice_mask` on one device may be relied on, other than what follows from the above.
Results may differ from a plain program's by a relative error of at most 0.0003.
Values sent between devices are 32-bit elements; how exact they have to be, the bound alone decides.
A program may use at most 64 MiB of HBM per device.

v0:
```python
import jax
import jax.numpy as jnp
from jax import lax
from jax.sharding import PartitionSpec as P

bed_unit = 2.0 ** (-29)
factor_u = (2.0, 1.0, 0.5)
factor_v = (2.0, 0.5, 1.0)


def extended_2(cells, sides, width):
    for axis, dim in sides:
        count = lax.axis_size(axis)
        ends = count - 1
        head = lax.slice_in_dim(cells, 0, width, axis=dim)
        tail = lax.slice_in_dim(cells, cells.shape[dim] - width, cells.shape[dim], axis=dim)
        cells = jnp.concatenate(
            [
                lax.ppermute(tail, axis, [(i, (i + 1) % count) for i in range(ends)]),
                cells,
                lax.ppermute(head, axis, [((i + 1) % count, i) for i in range(ends)]),
            ],
            axis=dim,
        )
    return cells


def coefficient(offset):
    nonzero = len([entry for entry in offset if entry != 0])
    weight_u = 0.25 ** (nonzero - 1)
    weight_v = weight_u
    for dimension in range(3):
        if offset[dimension] != 0:
            weight_u = weight_u * factor_u[dimension]
            weight_v = weight_v * factor_v[dimension]
    return jnp.array([weight_u, weight_v], jnp.float32).reshape(2, 1, 1, 1)


def neighbour_sum(padded):
    layers = padded.shape[-3] - 2
    span_x = padded.shape[-2] - 2
    span_y = padded.shape[-1] - 2
    summed = None
    for step_z in (-1, 0, 1):
        for step_x in (-1, 0, 1):
            for step_y in (-1, 0, 1):
                if step_z == 0 and step_x == 0 and (step_y == 0):
                    continue
                window = padded[
                    ...,
                    1 + step_z : 1 + step_z + layers,
                    1 + step_x : 1 + step_x + span_x,
                    1 + step_y : 1 + step_y + span_y,
                ]
                addend = coefficient((step_z, step_x, step_y)) * window
                summed = addend if summed is None else summed + addend
    return summed


def strain_roots(extended):
    padded = jnp.pad(extended, [(0, 0)] * (extended.ndim - 3) + [(1, 1), (0, 0), (0, 0)])
    along_x = (padded[..., 1:-1, 2:, 1:-1] - padded[..., 1:-1, :-2, 1:-1]) * 0.5
    along_y = (padded[..., 1:-1, 1:-1, 2:] - padded[..., 1:-1, 1:-1, :-2]) * 0.5
    along_z = (padded[..., 2:, 1:-1, 1:-1] - padded[..., :-2, 1:-1, 1:-1]) * 0.5
    stretch_x = along_x[..., 0, :, :, :]
    stretch_y = along_y[..., 1, :, :, :]
    shear_one = along_y[..., 0, :, :, :]
    shear_two = along_x[..., 1, :, :, :]
    vertical_u = along_z[..., 0, :, :, :]
    vertical_v = along_z[..., 1, :, :, :]
    shear = shear_one + shear_two
    strain = (
        stretch_x * stretch_x
        + stretch_y * stretch_y
        + stretch_x * stretch_y
        + 0.25 * shear * shear
        + 0.25 * (vertical_u * vertical_u + vertical_v * vertical_v)
    )
    return jnp.power(strain + 0.1, -1.0 / 6.0)[..., None, :, :, :]


def pad_layers(field):
    return jnp.pad(field, ((0, 0), (0, 0), (1, 1), (0, 0), (0, 0)))


def inner(left, right):
    return jnp.sum(left * right, axis=(1, 2, 3, 4))


def spread(values):
    return values.reshape(-1, 1, 1, 1, 1)


def trimmed(field, margin):
    return field[..., margin:-margin, margin:-margin]


def apply_local(roots_wide, across_part, diag_part, field_wide):
    product = roots_wide * field_wide
    nearby = neighbour_sum(pad_layers(product))
    centre = trimmed(field_wide, 1)
    return trimmed(roots_wide, 1) * (across_part * centre - nearby) + diag_part * centre


def body(u_prior, friction_rows, friction_table, bed_fixed, ice_mask):
    members = u_prior.shape[0]
    layers = u_prior.shape[2]
    rows_x = u_prior.shape[3]
    rows_y = u_prior.shape[4]
    total_x = rows_x * lax.axis_size("plane")
    cover = ice_mask.astype(jnp.float32)
    bed_block = (bed_fixed.astype(jnp.float32) * bed_unit).reshape(1, 1, 1, rows_x, rows_y)
    levels = jnp.arange(friction_table.shape[0], dtype=jnp.int32)
    chosen = (friction_rows[:, None] == levels[None, :]).astype(jnp.float32)
    friction = jnp.sum(chosen[:, :, None, None] * friction_table[None], axis=1)
    bottom = (
        (jnp.arange(layers, dtype=jnp.int32) == 0).astype(jnp.float32).reshape(1, 1, layers, 1, 1)
    )
    mask_block = cover.reshape(1, 1, 1, rows_x, rows_y)
    friction_block = friction.reshape(members, 1, 1, rows_x, rows_y)
    prior_wide, bed_wide, mask_wide, friction_wide = (
        extended_2(u_prior, (("plane", 3), ("planey", 4)), 4),
        extended_2(bed_block, (("plane", 3), ("planey", 4)), 4),
        extended_2(mask_block, (("plane", 3), ("planey", 4)), 4),
        extended_2(friction_block, (("plane", 3), ("planey", 4)), 4),
    )
    roots_three = trimmed(mask_wide, 1) * strain_roots(prior_wide)
    across_two = neighbour_sum(pad_layers(roots_three))
    bed_three = trimmed(bed_wide, 1)
    slope_x = (bed_three[..., 2:, 1:-1] - bed_three[..., :-2, 1:-1]) * 0.5
    slope_y = (bed_three[..., 1:-1, 2:] - bed_three[..., 1:-1, :-2]) * 0.5
    mask_two = trimmed(mask_wide, 2)
    position = (
        lax.axis_index("plane") * rows_x - 2 + jnp.arange(rows_x + 4, dtype=jnp.int32)
    ).astype(jnp.float32)
    thickness = 1.0 + 2.0 * position[:, None] / (total_x - 1)
    force_two = jnp.concatenate(
        [-(mask_two * thickness * slope_x), -(mask_two * thickness * slope_y)], axis=1
    )
    diag_two = mask_two * trimmed(friction_wide, 2) * bottom + (1.0 - mask_two)
    start_three = trimmed(prior_wide, 1) * trimmed(mask_wide, 1)
    residual_two = force_two - apply_local(roots_three, across_two, diag_two, start_three)
    image_one = apply_local(
        trimmed(roots_three, 1), trimmed(across_two, 1), trimmed(diag_two, 1), residual_two
    )
    second_image = apply_local(
        trimmed(roots_three, 2), trimmed(across_two, 2), trimmed(diag_two, 2), image_one
    )
    residual = trimmed(residual_two, 2)
    image = trimmed(image_one, 1)
    gram_rr, gram_ra, gram_aa, gram_ab = lax.psum(
        (
            inner(residual, residual),
            inner(residual, image),
            inner(image, image),
            inner(image, second_image),
        ),
        ("plane", "planey"),
    )
    first_step = gram_rr / gram_ra
    norm_next = gram_rr - 2.0 * first_step * gram_ra + first_step * first_step * gram_aa
    growth = 1.0 + norm_next / gram_rr
    curve = (
        growth * growth * gram_ra
        - 2.0 * growth * first_step * gram_aa
        + first_step * first_step * gram_ab
    )
    second_step = norm_next / curve
    solution = trimmed(start_three, 3)
    solution = (
        solution
        + spread(first_step + second_step * growth) * residual
        - spread(second_step * first_step) * image
    )
    local_sum = jnp.sum(solution, axis=0)
    summed = lax.psum(local_sum, "ens")
    return summed / (members * lax.axis_size("ens"))


def solution(mesh):
    in_specs = (
        P(("group", "ens"), None, None, "plane", "planey"),
        P(("group", "ens")),
        P("group", "plane", "planey"),
        P("plane", "planey"),
        P("plane", "planey"),
    )
    out_specs = P("group", None, "plane", "planey")
    return jax.shard_map(body, mesh=mesh, in_specs=in_specs, out_specs=out_specs, check_vma=False)
```

profile of v0, /device:TPU:0, one launch (start us, length us, event | category | flops | bytes accessed | tf_op | source)
XLA Modules:
  0.0 144.7 jit_solution(11222235841737665456)
XLA Ops:
  6.5 0.7 convert_bitcast_fusion
  7.2 4.9 %collective-permute-start.4 = (f32[1,1,1,4,128]{4,3,2,1,0:T(4,128)S(1)}, f32[1,1,1,4,128]{4,3,2,1,0:T(4,128)S(1)}, u32[]{:S(2)}, u32[]{:S(2)}) collective-permute-start(f32[1,1,1,4,128]{4,3,2,1,0:T(4,128)S(1)} %get-tuple-element.72), channel_id=1, source_target_pairs={{0,4},{4,8},{8,12},{1,5},{5,9},{9,13},{2,6},{6,10},{10,14},{3,7},{... | collective-permute-start | bytes 6152 | tf_op jit(solution)/shard_map/ppermute | solution.py:19
  12.2 1.3 collective-permute-start.5
  13.5 0.7 multiply_bitcast_fusion
  14.2 4.5 %collective-permute-start.8 = (f32[1,1,1,4,128]{4,3,2,1,0:T(4,128)S(1)}, f32[1,1,1,4,128]{4,3,2,1,0:T(4,128)S(1)}, u32[]{:S(2)}, u32[]{:S(2)}) collective-permute-start(f32[1,1,1,4,128]{4,3,2,1,0:T(4,128)S(1)} %get-tuple-element.70), channel_id=1, source_target_pairs={{0,4},{4,8},{8,12},{1,5},{5,9},{9,13},{2,6},{6,10},{10,14},{3,7},{... | collective-permute-start | bytes 6152 | tf_op jit(solution)/shard_map/ppermute | solution.py:19
  18.7 1.3 collective-permute-start.9
  20.0 0.7 compare_convert_fusion.1
  20.8 1.0 multiply_reduce_fusion.3
  21.8 4.5 %collective-permute-start.12 = (f32[2,1,1,4,128]{4,3,0,2,1:T(4,128)S(1)}, f32[2,1,1,4,128]{4,3,0,2,1:T(4,128)S(1)}, u32[]{:S(2)}, u32[]{:S(2)}) collective-permute-start(f32[2,1,1,4,128]{4,3,0,2,1:T(4,128)S(1)} %get-tuple-element.64), channel_id=1, source_target_pairs={{0,4},{4,8},{8,12},{1,5},{5,9},{9,13},{2,6},{6,10},{10,14},{3,7},{... | collective-permute-start | bytes 12296 | tf_op jit(solution)/shard_map/ppermute | solution.py:19
  26.4 1.0 fusion.197
  27.4 1.3 collective-permute-start.13
  28.7 4.6 %collective-permute-start = (f32[2,2,10,4,128]{4,3,2,1,0:T(4,128)S(1)}, f32[2,2,10,4,128]{4,3,2,1,0:T(4,128)S(1)}, u32[]{:S(2)}, u32[]{:S(2)}) collective-permute-start(f32[2,2,10,4,128]{4,3,2,1,0:T(4,128)S(1)} %get-tuple-element.56), channel_id=1, source_target_pairs={{0,4},{4,8},{8,12},{1,5},{5,9},{9,13},{2,6},{6,10},{10,14},{3,7},{... | collective-permute-start | bytes 245768 | tf_op jit(solution)/shard_map/ppermute | solution.py:19
  33.3 0.1 fusion.201
  33.4 3.4 %collective-permute-start.6 = (f32[1,1,1,24,4]{4,3,2,1,0:T(8,128)S(1)}, f32[1,1,1,24,4]{4,3,2,1,0:T(8,128)S(1)}, u32[]{:S(2)}, u32[]{:S(2)}) collective-permute-start(f32[1,1,1,24,4]{4,3,2,1,0:T(8,128)S(1)} %get-tuple-element.68), channel_id=1, source_target_pairs={{0,2},{1,3},{4,6},{5,7},{8,10},{9,11},{12,14},{13,15},{16,18},{17,... | collective-permute-start | bytes 1160 | tf_op jit(solution)/shard_map/ppermute | solution.py:19
  36.8 1.3 collective-permute-start.7
  38.1 0.1 fusion.200
  38.2 4.5 %collective-permute-start.10 = (f32[1,1,1,24,4]{4,3,2,1,0:T(8,128)S(1)}, f32[1,1,1,24,4]{4,3,2,1,0:T(8,128)S(1)}, u32[]{:S(2)}, u32[]{:S(2)}) collective-permute-start(f32[1,1,1,24,4]{4,3,2,1,0:T(8,128)S(1)} %get-tuple-element.66), channel_id=1, source_target_pairs={{0,2},{1,3},{4,6},{5,7},{8,10},{9,11},{12,14},{13,15},{16,18},{17,... | collective-permute-start | bytes 1160 | tf_op jit(solution)/shard_map/ppermute | solution.py:19
  42.7 1.3 collective-permute-start.11
  44.0 0.1 pad_maximum_fusion.6
  44.1 0.0 collective-permute-done.10
  44.1 1.3 collective-permute-start.1
  45.4 2.9 %collective-permute-done.11 = f32[1,1,1,24,4]{4,3,2,1,0:T(8,128)S(1)} collective-permute-done((f32[1,1,1,24,4]{4,3,2,1,0:T(8,128)S(1)}, f32[1,1,1,24,4]{4,3,2,1,0:T(8,128)S(1)}, u32[]{:S(2)}, u32[]{:S(2)}) %collective-permute-start.11) | collective-permute-done | bytes 416 | tf_op jit(solution)/shard_map/ppermute | solution.py:21
  48.3 0.1 pad_maximum_fusion.7
  48.4 0.1 fusion.193
  48.5 0.1 slice_bitcast_fusion.9
  48.6 0.1 fusion.198
  48.7 1.6 %collective-permute-start.14 = (f32[2,1,1,24,4]{4,3,0,2,1:T(8,128)S(1)}, f32[2,1,1,24,4]{4,3,0,2,1:T(8,128)S(1)}, u32[]{:S(2)}, u32[]{:S(2)}) collective-permute-start(f32[2,1,1,24,4]{4,3,0,2,1:T(8,128)S(1)} %get-tuple-element.62), channel_id=1, source_target_pairs={{0,2},{1,3},{4,6},{5,7},{8,10},{9,11},{12,14},{13,15},{16,18},{17,... | collective-permute-start | bytes 2312 | tf_op jit(solution)/shard_map/ppermute | solution.py:19
  50.4 1.3 collective-permute-start.15
  51.7 0.2 collective-permute-done.14
  51.9 4.2 %collective-permute-done.15 = f32[2,1,1,24,4]{4,3,0,2,1:T(8,128)S(1)} collective-permute-done((f32[2,1,1,24,4]{4,3,0,2,1:T(8,128)S(1)}, f32[2,1,1,24,4]{4,3,0,2,1:T(8,128)S(1)}, u32[]{:S(2)}, u32[]{:S(2)}) %collective-permute-start.15) | collective-permute-done | bytes 800 | tf_op jit(solution)/shard_map/ppermute | solution.py:21
  56.1 0.1 fusion.187
  56.2 0.0 copy-start
  56.2 0.1 multiply_add_fusion
  56.3 0.2 slice_bitcast_fusion
  56.5 0.1 multiply_add_fusion.1
  56.7 0.5 copy-done
  57.2 0.1 pad_maximum_fusion.1
  57.2 0.2 fusion.196
  57.4 1.7 %collective-permute-start.2 = (f32[2,2,10,24,4]{4,3,2,1,0:T(8,128)S(1)}, f32[2,2,10,24,4]{4,3,2,1,0:T(8,128)S(1)}, u32[]{:S(2)}, u32[]{:S(2)}) collective-permute-start(f32[2,2,10,24,4]{4,3,2,1,0:T(8,128)S(1)} %get-tuple-element.54), channel_id=1, source_target_pairs={{0,2},{1,3},{4,6},{5,7},{8,10},{9,11},{12,14},{13,15},{16,18},{17,... | collective-permute-start | bytes 46088 | tf_op jit(solution)/shard_map/ppermute | solution.py:19
  59.1 1.3 collective-permute-start.3
  60.4 0.1 slice_bitcast_fusion.7
  60.5 4.9 %collective-permute-done.2 = f32[2,2,10,24,4]{4,3,2,1,0:T(8,128)S(1)} collective-permute-done((f32[2,2,10,24,4]{4,3,2,1,0:T(8,128)S(1)}, f32[2,2,10,24,4]{4,3,2,1,0:T(8,128)S(1)}, u32[]{:S(2)}, u32[]{:S(2)}) %collective-permute-start.2) | collective-permute-done | bytes 15392 | tf_op jit(solution)/shard_map/ppermute | solution.py:19
  65.4 4.4 %collective-permute-done.3 = f32[2,2,10,24,4]{4,3,2,1,0:T(8,128)S(1)} collective-permute-done((f32[2,2,10,24,4]{4,3,2,1,0:T(8,128)S(1)}, f32[2,2,10,24,4]{4,3,2,1,0:T(8,128)S(1)}, u32[]{:S(2)}, u32[]{:S(2)}) %collective-permute-start.3) | collective-permute-done | bytes 15392 | tf_op jit(solution)/shard_map/ppermute | solution.py:21
  69.8 0.6 pad_maximum_fusion
  70.5 1.3 fusion.95
  71.8 0.5 fusion.101
  72.3 5.0 %fusion.103 = (f32[2,10,20,132]{3,2,1,0:T(8,128)S(1)}, f32[2,10,20,132]{3,2,1,0:T(8,128)}, f32[2,10,20,132]{3,2,1,0:T(8,128)}, f32[2,10,20,132]{3,2,1,0:T(8,128)...) fusion(f32[2,1,10,22,134]{4,3,2,1,0:T(8,128)S(1)} %fusion.101), kind=kLoop, calls=%fused_computation.200 | loop fusion | flops 580800 | bytes 4995840 | tf_op jit(solution)/shard_map/mul | solution.py:55
  77.3 2.6 %fusion.133 = (f32[2,10,20,132]{3,2,1,0:T(8,128)}, f32[2,10,20,132]{3,2,1,0:T(8,128)}, f32[2,10,20,132]{3,2,1,0:T(8,128)}, f32[2,10,20,132]{3,2,1,0:T(8,128)}, f...) fusion(f32[2,1,10,22,134]{4,3,2,1,0:T(8,128)S(1)} %fusion.101), kind=kLoop, calls=%fused_computation.240 | loop fusion | flops 158400 | bytes 3379200 | tf_op jit(solution)/shard_map/mul | solution.py:55
  79.9 1.0 slice_bitcast_fusion.1
  80.9 0.8 slice_bitcast_fusion.8
  81.7 0.3 broadcast_multiply_fusion.1
  82.0 0.3 copy-done.2
  82.3 0.0 copy-done.3
  82.3 0.0 copy-done.4
  82.4 0.0 copy-done.5
  82.4 8.9 %broadcast_multiply_fusion.2 = (f32[2,2,10,20,132]{4,3,2,1,0:T(8,128)S(1)}, f32[2,2,10,20,132]{4,3,2,1,0:T(8,128)S(1)}, f32[2,2,10,20,132]{4,3,2,1,0:T(8,128)S(1)}) fusion(f32[2,10,20,132]{3,2,1,0:T(8,128)} %get-tuple-element.53, f32[2,10,20,132]{3,2,1,0:T(8,128)S(1)} %multiply_add_fusion.1, f32[2,2,10,22,134]{4,3,2,1,0:T(8,128)S(1)} %get-tuple-element.21, ...), kind=kLoop, calls=%fused_computation.252 | loop fusion | flops 10032000 | bytes 17623040 | tf_op jit(solution)/shard_map/mul | solution.py:99
  91.3 0.0 copy-start.1
  91.3 5.9 %broadcast_multiply_fusion = (f32[2,2,10,18,130]{4,3,2,1,0:T(8,128)S(1)}, f32[2,2,10,18,130]{4,3,2,1,0:T(8,128)S(1)}) fusion(f32[2,10,18,130]{3,2,1,0:T(8,128)} %slice_bitcast_fusion.1, f32[2,10,18,130]{3,2,1,0:T(8,128)S(1)} %slice_bitcast_fusion, f32[2,2,10,20,132]{4,3,2,1,0:T(8,128)S(1)} %get-tuple-element.18, f32[2]{0:T(128)S(1)} %copy-done.5, ...), kind=kLoop, calls=%fused_computation.249 | loop fusion | flops 5335200 | bytes 12243008 | tf_op jit(solution)/shard_map/mul | solution.py:99
  97.2 1.8 %multiply_reduce_fusion.1 = (f32[2]{0:T(128)S(1)}, f32[2]{0:T(128)S(1)}, f32[2]{0:T(128)S(1)}, f32[2]{0:T(128)S(1)}) fusion(f32[2,2,10,20,132]{4,3,2,1,0:T(8,128)S(1)} %get-tuple-element.19, f32[2,2,10,18,130]{4,3,2,1,0:T(8,128)S(1)} %get-tuple-element.17, f32[2,10,16,128]{3,2,1,0:T(8,128)S(1)} %slice_bitcast_fusion.7, ...), kind=kLoop, calls=%fused_computation.313 | loop fusion | flops 5242872 | bytes 4917280 | tf_op jit(solution)/shard_map/reduce_sum | solution.py:87
  99.0 20.8 %all-reduce.5 = (f32[2]{0:T(128)S(1)}, f32[2]{0:T(128)S(1)}, f32[2]{0:T(128)S(1)}, f32[2]{0:T(128)S(1)}) all-reduce(f32[2]{0:T(128)S(1)} %get-tuple-element.23, f32[2]{0:T(128)S(1)} %get-tuple-element.6, f32[2]{0:T(128)S(1)} %get-tuple-element.7, ...), channel_id=1, replica_groups=mesh['group'=2,'plane'=4,'planey'=2,'ens'=2] {'plane','planey'}, use_global_device_ids=true, to_apply=%region_8.9 | all-reduce | flops 8 | bytes 64 | tf_op jit(solution)/shard_map/psum | solution.py:151
  119.8 1.0 fusion.184
  120.8 0.0 all-reduce.8.cloned.1.call-update
  120.8 15.4 %all-reduce.8.cloned.1.call-done = f32[2,10,16,128]{3,2,1,0:T(8,128)} async-done(((f32[2,10,16,128]{3,2,1,0:T(8,128)}), f32[2,10,16,128]{3,2,1,0:T(8,128)}) %all-reduce.8.cloned.1.call-update) | async-done | bytes 163856 | tf_op jit(solution)/shard_map/psum | solution.py:176
  136.3 1.6 %broadcast_multiply_fusion.3 = f32[2,10,16,128]{3,2,1,0:T(8,128)} fusion(f32[2,10,16,128]{3,2,1,0:T(8,128)} %all-reduce.8.cloned.1.call-done), kind=kLoop, calls=%fused_computation.319 | loop fusion | flops 40960 | bytes 327680 | tf_op jit(solution)/shard_map/div | solution.py:177
  (28 shorter events, 0.1 us)
Async XLA Ops:
  6.5 129.7 %all-reduce.8.cloned.1.call-start = ((), (), s32[]{:S(2)}) async-start(), calls=%async_computation | async-start | bytes 327680 | tf_op jit(solution)/shard_map/psum | solution.py:176
  7.2 20.2 %collective-permute-start.4 = (f32[1,1,1,4,128]{4,3,2,1,0:T(4,128)S(1)}, f32[1,1,1,4,128]{4,3,2,1,0:T(4,128)S(1)}, u32[]{:S(2)}, u32[]{:S(2)}) collective-permute-start(f32[1,1,1,4,128]{4,3,2,1,0:T(4,128)S(1)} %get-tuple-element.72), channel_id=1, source_target_pairs={{0,4},{4,8},{8,12},{1,5},{5,9},{9,13},{2,6},{6,10},{10,14},{3,7},{... | collective-permute-start | bytes 6152 | tf_op jit(solution)/shard_map/ppermute | solution.py:19
  12.2 16.5 %collective-permute-start.5 = (f32[1,1,1,4,128]{4,3,2,1,0:T(4,128)S(1)}, f32[1,1,1,4,128]{4,3,2,1,0:T(4,128)S(1)}, u32[]{:S(2)}, u32[]{:S(2)}) collective-permute-start(f32[1,1,1,4,128]{4,3,2,1,0:T(4,128)S(1)} %get-tuple-element.73), channel_id=1, source_target_pairs={{4,0},{8,4},{12,8},{5,1},{9,5},{13,9},{6,2},{10,6},{14,10},{7,3},{... | collective-permute-start | bytes 6152 | tf_op jit(solution)/shard_map/ppermute | solution.py:21
  14.2 19.2 %collective-permute-start.8 = (f32[1,1,1,4,128]{4,3,2,1,0:T(4,128)S(1)}, f32[1,1,1,4,128]{4,3,2,1,0:T(4,128)S(1)}, u32[]{:S(2)}, u32[]{:S(2)}) collective-permute-start(f32[1,1,1,4,128]{4,3,2,1,0:T(4,128)S(1)} %get-tuple-element.70), channel_id=1, source_target_pairs={{0,4},{4,8},{8,12},{1,5},{5,9},{9,13},{2,6},{6,10},{10,14},{3,7},{... | collective-permute-start | bytes 6152 | tf_op jit(solution)/shard_map/ppermute | solution.py:19
  18.7 18.0 %collective-permute-start.9 = (f32[1,1,1,4,128]{4,3,2,1,0:T(4,128)S(1)}, f32[1,1,1,4,128]{4,3,2,1,0:T(4,128)S(1)}, u32[]{:S(2)}, u32[]{:S(2)}) collective-permute-start(f32[1,1,1,4,128]{4,3,2,1,0:T(4,128)S(1)} %get-tuple-element.71), channel_id=1, source_target_pairs={{4,0},{8,4},{12,8},{5,1},{9,5},{13,9},{6,2},{10,6},{14,10},{7,3},{... | collective-permute-start | bytes 6152 | tf_op jit(solution)/shard_map/ppermute | solution.py:21
  21.8 26.8 %collective-permute-start.12 = (f32[2,1,1,4,128]{4,3,0,2,1:T(4,128)S(1)}, f32[2,1,1,4,128]{4,3,0,2,1:T(4,128)S(1)}, u32[]{:S(2)}, u32[]{:S(2)}) collective-permute-start(f32[2,1,1,4,128]{4,3,0,2,1:T(4,128)S(1)} %get-tuple-element.64), channel_id=1, source_target_pairs={{0,4},{4,8},{8,12},{1,5},{5,9},{9,13},{2,6},{6,10},{10,14},{3,7},{... | collective-permute-start | bytes 12296 | tf_op jit(solution)/shard_map/ppermute | solution.py:19
  27.4 21.2 %collective-permute-start.13 = (f32[2,1,1,4,128]{4,3,0,2,1:T(4,128)S(1)}, f32[2,1,1,4,128]{4,3,0,2,1:T(4,128)S(1)}, u32[]{:S(2)}, u32[]{:S(2)}) collective-permute-start(f32[2,1,1,4,128]{4,3,0,2,1:T(4,128)S(1)} %get-tuple-element.65), channel_id=1, source_target_pairs={{4,0},{8,4},{12,8},{5,1},{9,5},{13,9},{6,2},{10,6},{14,10},{7,3},{... | collective-permute-start | bytes 12296 | tf_op jit(solution)/shard_map/ppermute | solution.py:21
  28.7 27.9 %collective-permute-start = (f32[2,2,10,4,128]{4,3,2,1,0:T(4,128)S(1)}, f32[2,2,10,4,128]{4,3,2,1,0:T(4,128)S(1)}, u32[]{:S(2)}, u32[]{:S(2)}) collective-permute-start(f32[2,2,10,4,128]{4,3,2,1,0:T(4,128)S(1)} %get-tuple-element.56), channel_id=1, source_target_pairs={{0,4},{4,8},{8,12},{1,5},{5,9},{9,13},{2,6},{6,10},{10,14},{3,7},{... | collective-permute-start | bytes 245768 | tf_op jit(solution)/shard_map/ppermute | solution.py:19
  33.4 4.8 %collective-permute-start.6 = (f32[1,1,1,24,4]{4,3,2,1,0:T(8,128)S(1)}, f32[1,1,1,24,4]{4,3,2,1,0:T(8,128)S(1)}, u32[]{:S(2)}, u32[]{:S(2)}) collective-permute-start(f32[1,1,1,24,4]{4,3,2,1,0:T(8,128)S(1)} %get-tuple-element.68), channel_id=1, source_target_pairs={{0,2},{1,3},{4,6},{5,7},{8,10},{9,11},{12,14},{13,15},{16,18},{17,... | collective-permute-start | bytes 1160 | tf_op jit(solution)/shard_map/ppermute | solution.py:19
  36.8 5.9 %collective-permute-start.7 = (f32[1,1,1,24,4]{4,3,2,1,0:T(8,128)S(1)}, f32[1,1,1,24,4]{4,3,2,1,0:T(8,128)S(1)}, u32[]{:S(2)}, u32[]{:S(2)}) collective-permute-start(f32[1,1,1,24,4]{4,3,2,1,0:T(8,128)S(1)} %get-tuple-element.69), channel_id=1, source_target_pairs={{2,0},{3,1},{6,4},{7,5},{10,8},{11,9},{14,12},{15,13},{18,16},{19,... | collective-permute-start | bytes 1160 | tf_op jit(solution)/shard_map/ppermute | solution.py:21
  38.2 5.9 %collective-permute-start.10 = (f32[1,1,1,24,4]{4,3,2,1,0:T(8,128)S(1)}, f32[1,1,1,24,4]{4,3,2,1,0:T(8,128)S(1)}, u32[]{:S(2)}, u32[]{:S(2)}) collective-permute-start(f32[1,1,1,24,4]{4,3,2,1,0:T(8,128)S(1)} %get-tuple-element.66), channel_id=1, source_target_pairs={{0,2},{1,3},{4,6},{5,7},{8,10},{9,11},{12,14},{13,15},{16,18},{17,... | collective-permute-start | bytes 1160 | tf_op jit(solution)/shard_map/ppermute | solution.py:19
  42.7 5.6 %collective-permute-start.11 = (f32[1,1,1,24,4]{4,3,2,1,0:T(8,128)S(1)}, f32[1,1,1,24,4]{4,3,2,1,0:T(8,128)S(1)}, u32[]{:S(2)}, u32[]{:S(2)}) collective-permute-start(f32[1,1,1,24,4]{4,3,2,1,0:T(8,128)S(1)} %get-tuple-element.67), channel_id=1, source_target_pairs={{2,0},{3,1},{6,4},{7,5},{10,8},{11,9},{14,12},{15,13},{18,16},{19,... | collective-permute-start | bytes 1160 | tf_op jit(solution)/shard_map/ppermute | solution.py:21
  44.1 12.5 %collective-permute-start.1 = (f32[2,2,10,4,128]{4,3,2,1,0:T(4,128)S(1)}, f32[2,2,10,4,128]{4,3,2,1,0:T(4,128)S(1)}, u32[]{:S(2)}, u32[]{:S(2)}) collective-permute-start(f32[2,2,10,4,128]{4,3,2,1,0:T(4,128)S(1)} %get-tuple-element.57), channel_id=1, source_target_pairs={{4,0},{8,4},{12,8},{5,1},{9,5},{13,9},{6,2},{10,6},{14,10},{7,3},{... | collective-permute-start | bytes 245768 | tf_op jit(solution)/shard_map/ppermute | solution.py:21
  48.7 3.2 %collective-permute-start.14 = (f32[2,1,1,24,4]{4,3,0,2,1:T(8,128)S(1)}, f32[2,1,1,24,4]{4,3,0,2,1:T(8,128)S(1)}, u32[]{:S(2)}, u32[]{:S(2)}) collective-permute-start(f32[2,1,1,24,4]{4,3,0,2,1:T(8,128)S(1)} %get-tuple-element.62), channel_id=1, source_target_pairs={{0,2},{1,3},{4,6},{5,7},{8,10},{9,11},{12,14},{13,15},{16,18},{17,... | collective-permute-start | bytes 2312 | tf_op jit(solution)/shard_map/ppermute | solution.py:19
  50.4 5.7 %collective-permute-start.15 = (f32[2,1,1,24,4]{4,3,0,2,1:T(8,128)S(1)}, f32[2,1,1,24,4]{4,3,0,2,1:T(8,128)S(1)}, u32[]{:S(2)}, u32[]{:S(2)}) collective-permute-start(f32[2,1,1,24,4]{4,3,0,2,1:T(8,128)S(1)} %get-tuple-element.63), channel_id=1, source_target_pairs={{2,0},{3,1},{6,4},{7,5},{10,8},{11,9},{14,12},{15,13},{18,16},{19,... | collective-permute-start | bytes 2312 | tf_op jit(solution)/shard_map/ppermute | solution.py:21
  56.2 1.0 copy-start
  57.4 8.0 %collective-permute-start.2 = (f32[2,2,10,24,4]{4,3,2,1,0:T(8,128)S(1)}, f32[2,2,10,24,4]{4,3,2,1,0:T(8,128)S(1)}, u32[]{:S(2)}, u32[]{:S(2)}) collective-permute-start(f32[2,2,10,24,4]{4,3,2,1,0:T(8,128)S(1)} %get-tuple-element.54), channel_id=1, source_target_pairs={{0,2},{1,3},{4,6},{5,7},{8,10},{9,11},{12,14},{13,15},{16,18},{17,... | collective-permute-start | bytes 46088 | tf_op jit(solution)/shard_map/ppermute | solution.py:19
  59.1 10.7 %collective-permute-start.3 = (f32[2,2,10,24,4]{4,3,2,1,0:T(8,128)S(1)}, f32[2,2,10,24,4]{4,3,2,1,0:T(8,128)S(1)}, u32[]{:S(2)}, u32[]{:S(2)}) collective-permute-start(f32[2,2,10,24,4]{4,3,2,1,0:T(8,128)S(1)} %get-tuple-element.55), channel_id=1, source_target_pairs={{2,0},{3,1},{6,4},{7,5},{10,8},{11,9},{14,12},{15,13},{18,16},{19,... | collective-permute-start | bytes 46088 | tf_op jit(solution)/shard_map/ppermute | solution.py:21
  81.7 0.7 copy-start.2
  81.7 0.7 copy-start.3
  81.7 0.7 copy-start.4
  81.7 0.7 copy-start.5
  91.3 5.9 %copy-start.1 = (f32[2,10,16,128]{3,2,1,0:T(8,128)S(1)}, f32[2,10,16,128]{3,2,1,0:T(8,128)}, u32[]{:S(2)}) copy-start(f32[2,10,16,128]{3,2,1,0:T(8,128)} %slice_bitcast_fusion.8) | copy-start | bytes 491524
Sparse Core Ops, SparseCore 0:
  120.9 15.2 all-reduce.7
where the time goes:
time: 146 us; the launch traced here: 145 us
  starting transfers between devices  40.1 us (27%)
  other arithmetic  33.4 us (23%)
  waiting for transfers between devices  32.1 us (22%)
  blocking collectives  20.8 us (14%)
  between operations  13.8 us (9%)
  local copies, waits for them, and re-layouts  4.52 us (3%)
    ppermute x8, starting transfers between devices, extended_2(): lax.ppermute(tail, axis, [(i, (i + 1) % count) for i in range(ends)])  29.8 us
    psum x1, blocking collectives, body(): lax.psum((inner(residual, residual), inner(residual, image), inner(image,...  20.8 us
    psum x1, waiting for transfers between devices, body(): summed = lax.psum(local_sum, 'ens')  15.4 us
    mul x3, other arithmetic, apply_local(): product = roots_wide * field_wide  15.1 us
    ppermute x8, waiting for transfers between devices, extended_2(): lax.ppermute(head, axis, [((i + 1) % count, i) for i in range(ends)])  11.6 us
    ppermute x8, starting transfers between devices, extended_2(): lax.ppermute(head, axis, [((i + 1) % count, i) for i in range(ends)])  10.3 us
    mul x2, other arithmetic, neighbour_sum(): addend = coefficient((step_z, step_x, step_y)) * window  7.6 us
    ppermute x8, waiting for transfers between devices, extended_2(): lax.ppermute(tail, axis, [(i, (i + 1) % count) for i in range(ends)])  5.09 us
  transfers between devices with their start and end apart: 17, of which 6 were waited for; matrix products, arithmetic and copies ran while one was open for 3% of the time, Pallas kernels for 0%

commit v1 on v0

--- a/solution.py
+++ b/solution.py
@@ -173,7 +173,8 @@
         - spread(second_step * first_step) * image
     )
     local_sum = jnp.sum(solution, axis=0)
-    summed = lax.psum(local_sum, "ens")
+    terms = lax.all_gather(local_sum, "ens")
+    summed = jnp.sum(terms, axis=0)
     return summed / (members * lax.axis_size("ens"))
 
 

time: 146 us -> 117 us (0.80)
  waiting for transfers between devices: 32.1 us -> 16.6 us
  between operations: 13.8 us -> 0.4 us
  blocking collectives: 20.8 us -> 22.8 us
  other arithmetic: 33.4 us -> 31.8 us
    psum x1 -> x0, waiting for transfers between devices: 15.4 us -> none  [body(): summed = lax.psum(local_sum, 'ens')]
    all_gather x0 -> x1, blocking collectives: none -> 2.04 us  [body(): terms = lax.all_gather(local_sum, 'ens')]
  transfers between devices with their start and end apart: 17 -> 16, of which waited for: 6 -> 5; matrix products, arithmetic and copies ran while one was open for 3% -> 4% of each run, Pallas kernels for 0% -> 0%
where the time goes in v1:
time: 117 us; the launch traced here: 116 us
  starting transfers between devices  40.1 us (34%)
  other arithmetic  31.8 us (27%)
  blocking collectives  22.8 us (19%)
  waiting for transfers between devices  16.6 us (14%)
  local copies, waits for them, and re-layouts  4.52 us (4%)
    ppermute x8, starting transfers between devices, extended_2(): lax.ppermute(tail, axis, [(i, (i + 1) % count) for i in range(ends)])  29.8 us
    psum x1, blocking collectives, body(): lax.psum((inner(residual, residual), inner(residual, image), inner(image,...  20.8 us
    mul x3, other arithmetic, apply_local(): product = roots_wide * field_wide  15.1 us
    ppermute x8, waiting for transfers between devices, extended_2(): lax.ppermute(head, axis, [((i + 1) % count, i) for i in range(ends)])  11.6 us
    ppermute x8, starting transfers between devices, extended_2(): lax.ppermute(head, axis, [((i + 1) % count, i) for i in range(ends)])  10.3 us
    mul x2, other arithmetic, neighbour_sum(): addend = coefficient((step_z, step_x, step_y)) * window  7.59 us
    ppermute x8, waiting for transfers between devices, extended_2(): lax.ppermute(tail, axis, [(i, (i + 1) % count) for i in range(ends)])  5.09 us
  transfers between devices with their start and end apart: 16, of which 5 were waited for; matrix products, arithmetic and copies ran while one was open for 4% of the time, Pallas kernels for 0%

profile of v1, /device:TPU:0, one launch (start us, length us, event | category | flops | bytes accessed | tf_op | source)
XLA Modules:
  0.0 116.3 jit_solution(5246089524926820661)
XLA Ops:
  0.0 0.7 convert_bitcast_fusion
  0.7 4.9 %collective-permute-start.4 = (f32[1,1,1,4,128]{4,3,2,1,0:T(4,128)S(1)}, f32[1,1,1,4,128]{4,3,2,1,0:T(4,128)S(1)}, u32[]{:S(2)}, u32[]{:S(2)}) collective-permute-start(f32[1,1,1,4,128]{4,3,2,1,0:T(4,128)S(1)} %get-tuple-element.72), channel_id=1, source_target_pairs={{0,4},{4,8},{8,12},{1,5},{5,9},{9,13},{2,6},{6,10},{10,14},{3,7},{... | collective-permute-start | bytes 6152 | tf_op jit(solution)/shard_map/ppermute | solution.py:19
  5.7 1.3 %collective-permute-start.5 = (f32[1,1,1,4,128]{4,3,2,1,0:T(4,128)S(1)}, f32[1,1,1,4,128]{4,3,2,1,0:T(4,128)S(1)}, u32[]{:S(2)}, u32[]{:S(2)}) collective-permute-start(f32[1,1,1,4,128]{4,3,2,1,0:T(4,128)S(1)} %get-tuple-element.73), channel_id=1, source_target_pairs={{4,0},{8,4},{12,8},{5,1},{9,5},{13,9},{6,2},{10,6},{14,10},{7,3},{... | collective-permute-start | bytes 6152 | tf_op jit(solution)/shard_map/ppermute | solution.py:21
  7.0 0.7 multiply_bitcast_fusion
  7.7 4.5 %collective-permute-start.8 = (f32[1,1,1,4,128]{4,3,2,1,0:T(4,128)S(1)}, f32[1,1,1,4,128]{4,3,2,1,0:T(4,128)S(1)}, u32[]{:S(2)}, u32[]{:S(2)}) collective-permute-start(f32[1,1,1,4,128]{4,3,2,1,0:T(4,128)S(1)} %get-tuple-element.70), channel_id=1, source_target_pairs={{0,4},{4,8},{8,12},{1,5},{5,9},{9,13},{2,6},{6,10},{10,14},{3,7},{... | collective-permute-start | bytes 6152 | tf_op jit(solution)/shard_map/ppermute | solution.py:19
  12.2 1.3 %collective-permute-start.9 = (f32[1,1,1,4,128]{4,3,2,1,0:T(4,128)S(1)}, f32[1,1,1,4,128]{4,3,2,1,0:T(4,128)S(1)}, u32[]{:S(2)}, u32[]{:S(2)}) collective-permute-start(f32[1,1,1,4,128]{4,3,2,1,0:T(4,128)S(1)} %get-tuple-element.71), channel_id=1, source_target_pairs={{4,0},{8,4},{12,8},{5,1},{9,5},{13,9},{6,2},{10,6},{14,10},{7,3},{... | collective-permute-start | bytes 6152 | tf_op jit(solution)/shard_map/ppermute | solution.py:21
  13.5 0.7 compare_convert_fusion.1
  14.2 1.0 multiply_reduce_fusion.3
  15.3 4.5 %collective-permute-start.12 = (f32[2,1,1,4,128]{4,3,0,2,1:T(4,128)S(1)}, f32[2,1,1,4,128]{4,3,0,2,1:T(4,128)S(1)}, u32[]{:S(2)}, u32[]{:S(2)}) collective-permute-start(f32[2,1,1,4,128]{4,3,0,2,1:T(4,128)S(1)} %get-tuple-element.64), channel_id=1, source_target_pairs={{0,4},{4,8},{8,12},{1,5},{5,9},{9,13},{2,6},{6,10},{10,14},{3,7},{... | collective-permute-start | bytes 12296 | tf_op jit(solution)/shard_map/ppermute | solution.py:19
  19.8 1.0 fusion.197
  20.9 1.3 %collective-permute-start.13 = (f32[2,1,1,4,128]{4,3,0,2,1:T(4,128)S(1)}, f32[2,1,1,4,128]{4,3,0,2,1:T(4,128)S(1)}, u32[]{:S(2)}, u32[]{:S(2)}) collective-permute-start(f32[2,1,1,4,128]{4,3,0,2,1:T(4,128)S(1)} %get-tuple-element.65), channel_id=1, source_target_pairs={{4,0},{8,4},{12,8},{5,1},{9,5},{13,9},{6,2},{10,6},{14,10},{7,3},{... | collective-permute-start | bytes 12296 | tf_op jit(solution)/shard_map/ppermute | solution.py:21
  22.2 0.0 collective-permute-done.5
  22.2 4.6 %collective-permute-start = (f32[2,2,10,4,128]{4,3,2,1,0:T(4,128)S(1)}, f32[2,2,10,4,128]{4,3,2,1,0:T(4,128)S(1)}, u32[]{:S(2)}, u32[]{:S(2)}) collective-permute-start(f32[2,2,10,4,128]{4,3,2,1,0:T(4,128)S(1)} %get-tuple-element.56), channel_id=1, source_target_pairs={{0,4},{4,8},{8,12},{1,5},{5,9},{9,13},{2,6},{6,10},{10,14},{3,7},{... | collective-permute-start | bytes 245768 | tf_op jit(solution)/shard_map/ppermute | solution.py:19
  26.8 0.1 fusion.201
  26.9 3.4 %collective-permute-start.6 = (f32[1,1,1,24,4]{4,3,2,1,0:T(8,128)S(1)}, f32[1,1,1,24,4]{4,3,2,1,0:T(8,128)S(1)}, u32[]{:S(2)}, u32[]{:S(2)}) collective-permute-start(f32[1,1,1,24,4]{4,3,2,1,0:T(8,128)S(1)} %get-tuple-element.68), channel_id=1, source_target_pairs={{0,2},{1,3},{4,6},{5,7},{8,10},{9,11},{12,14},{13,15},{16,18},{17,... | collective-permute-start | bytes 1160 | tf_op jit(solution)/shard_map/ppermute | solution.py:19
  30.3 1.3 %collective-permute-start.7 = (f32[1,1,1,24,4]{4,3,2,1,0:T(8,128)S(1)}, f32[1,1,1,24,4]{4,3,2,1,0:T(8,128)S(1)}, u32[]{:S(2)}, u32[]{:S(2)}) collective-permute-start(f32[1,1,1,24,4]{4,3,2,1,0:T(8,128)S(1)} %get-tuple-element.69), channel_id=1, source_target_pairs={{2,0},{3,1},{6,4},{7,5},{10,8},{11,9},{14,12},{15,13},{18,16},{19,... | collective-permute-start | bytes 1160 | tf_op jit(solution)/shard_map/ppermute | solution.py:21
  31.6 0.1 fusion.200
  31.7 4.5 %collective-permute-start.10 = (f32[1,1,1,24,4]{4,3,2,1,0:T(8,128)S(1)}, f32[1,1,1,24,4]{4,3,2,1,0:T(8,128)S(1)}, u32[]{:S(2)}, u32[]{:S(2)}) collective-permute-start(f32[1,1,1,24,4]{4,3,2,1,0:T(8,128)S(1)} %get-tuple-element.66), channel_id=1, source_target_pairs={{0,2},{1,3},{4,6},{5,7},{8,10},{9,11},{12,14},{13,15},{16,18},{17,... | collective-permute-start | bytes 1160 | tf_op jit(solution)/shard_map/ppermute | solution.py:19
  36.2 1.3 %collective-permute-start.11 = (f32[1,1,1,24,4]{4,3,2,1,0:T(8,128)S(1)}, f32[1,1,1,24,4]{4,3,2,1,0:T(8,128)S(1)}, u32[]{:S(2)}, u32[]{:S(2)}) collective-permute-start(f32[1,1,1,24,4]{4,3,2,1,0:T(8,128)S(1)} %get-tuple-element.67), channel_id=1, source_target_pairs={{2,0},{3,1},{6,4},{7,5},{10,8},{11,9},{14,12},{15,13},{18,16},{19,... | collective-permute-start | bytes 1160 | tf_op jit(solution)/shard_map/ppermute | solution.py:21
  37.5 0.1 pad_maximum_fusion.6
  37.6 0.0 collective-permute-done.10
  37.6 1.3 %collective-permute-start.1 = (f32[2,2,10,4,128]{4,3,2,1,0:T(4,128)S(1)}, f32[2,2,10,4,128]{4,3,2,1,0:T(4,128)S(1)}, u32[]{:S(2)}, u32[]{:S(2)}) collective-permute-start(f32[2,2,10,4,128]{4,3,2,1,0:T(4,128)S(1)} %get-tuple-element.57), channel_id=1, source_target_pairs={{4,0},{8,4},{12,8},{5,1},{9,5},{13,9},{6,2},{10,6},{14,10},{7,3},{... | collective-permute-start | bytes 245768 | tf_op jit(solution)/shard_map/ppermute | solution.py:21
  38.9 2.9 %collective-permute-done.11 = f32[1,1,1,24,4]{4,3,2,1,0:T(8,128)S(1)} collective-permute-done((f32[1,1,1,24,4]{4,3,2,1,0:T(8,128)S(1)}, f32[1,1,1,24,4]{4,3,2,1,0:T(8,128)S(1)}, u32[]{:S(2)}, u32[]{:S(2)}) %collective-permute-start.11) | collective-permute-done | bytes 416 | tf_op jit(solution)/shard_map/ppermute | solution.py:21
  41.8 0.1 pad_maximum_fusion.7
  41.9 0.1 fusion.193
  42.0 0.1 slice_bitcast_fusion.9
  42.1 0.1 fusion.198
  42.2 1.6 %collective-permute-start.14 = (f32[2,1,1,24,4]{4,3,0,2,1:T(8,128)S(1)}, f32[2,1,1,24,4]{4,3,0,2,1:T(8,128)S(1)}, u32[]{:S(2)}, u32[]{:S(2)}) collective-permute-start(f32[2,1,1,24,4]{4,3,0,2,1:T(8,128)S(1)} %get-tuple-element.62), channel_id=1, source_target_pairs={{0,2},{1,3},{4,6},{5,7},{8,10},{9,11},{12,14},{13,15},{16,18},{17,... | collective-permute-start | bytes 2312 | tf_op jit(solution)/shard_map/ppermute | solution.py:19
  43.8 1.3 %collective-permute-start.15 = (f32[2,1,1,24,4]{4,3,0,2,1:T(8,128)S(1)}, f32[2,1,1,24,4]{4,3,0,2,1:T(8,128)S(1)}, u32[]{:S(2)}, u32[]{:S(2)}) collective-permute-start(f32[2,1,1,24,4]{4,3,0,2,1:T(8,128)S(1)} %get-tuple-element.63), channel_id=1, source_target_pairs={{2,0},{3,1},{6,4},{7,5},{10,8},{11,9},{14,12},{15,13},{18,16},{19,... | collective-permute-start | bytes 2312 | tf_op jit(solution)/shard_map/ppermute | solution.py:21
  45.1 0.2 collective-permute-done.14
  45.3 4.2 %collective-permute-done.15 = f32[2,1,1,24,4]{4,3,0,2,1:T(8,128)S(1)} collective-permute-done((f32[2,1,1,24,4]{4,3,0,2,1:T(8,128)S(1)}, f32[2,1,1,24,4]{4,3,0,2,1:T(8,128)S(1)}, u32[]{:S(2)}, u32[]{:S(2)}) %collective-permute-start.15) | collective-permute-done | bytes 800 | tf_op jit(solution)/shard_map/ppermute | solution.py:21
  49.5 0.1 fusion.187
  49.7 0.0 copy-start
  49.7 0.1 multiply_add_fusion
  49.8 0.2 slice_bitcast_fusion
  50.0 0.1 multiply_add_fusion.1
  50.1 0.5 copy-done
  50.6 0.1 pad_maximum_fusion.1
  50.7 0.2 fusion.196
  50.9 1.7 %collective-permute-start.2 = (f32[2,2,10,24,4]{4,3,2,1,0:T(8,128)S(1)}, f32[2,2,10,24,4]{4,3,2,1,0:T(8,128)S(1)}, u32[]{:S(2)}, u32[]{:S(2)}) collective-permute-start(f32[2,2,10,24,4]{4,3,2,1,0:T(8,128)S(1)} %get-tuple-element.54), channel_id=1, source_target_pairs={{0,2},{1,3},{4,6},{5,7},{8,10},{9,11},{12,14},{13,15},{16,18},{17,... | collective-permute-start | bytes 46088 | tf_op jit(solution)/shard_map/ppermute | solution.py:19
  52.6 1.3 %collective-permute-start.3 = (f32[2,2,10,24,4]{4,3,2,1,0:T(8,128)S(1)}, f32[2,2,10,24,4]{4,3,2,1,0:T(8,128)S(1)}, u32[]{:S(2)}, u32[]{:S(2)}) collective-permute-start(f32[2,2,10,24,4]{4,3,2,1,0:T(8,128)S(1)} %get-tuple-element.55), channel_id=1, source_target_pairs={{2,0},{3,1},{6,4},{7,5},{10,8},{11,9},{14,12},{15,13},{18,16},{19,... | collective-permute-start | bytes 46088 | tf_op jit(solution)/shard_map/ppermute | solution.py:21
  53.9 0.1 slice_bitcast_fusion.7
  54.0 4.9 %collective-permute-done.2 = f32[2,2,10,24,4]{4,3,2,1,0:T(8,128)S(1)} collective-permute-done((f32[2,2,10,24,4]{4,3,2,1,0:T(8,128)S(1)}, f32[2,2,10,24,4]{4,3,2,1,0:T(8,128)S(1)}, u32[]{:S(2)}, u32[]{:S(2)}) %collective-permute-start.2) | collective-permute-done | bytes 15392 | tf_op jit(solution)/shard_map/ppermute | solution.py:19
  58.9 4.4 %collective-permute-done.3 = f32[2,2,10,24,4]{4,3,2,1,0:T(8,128)S(1)} collective-permute-done((f32[2,2,10,24,4]{4,3,2,1,0:T(8,128)S(1)}, f32[2,2,10,24,4]{4,3,2,1,0:T(8,128)S(1)}, u32[]{:S(2)}, u32[]{:S(2)}) %collective-permute-start.3) | collective-permute-done | bytes 15392 | tf_op jit(solution)/shard_map/ppermute | solution.py:21
  63.3 0.6 pad_maximum_fusion
  63.9 1.3 %fusion.95 = (f32[2,2,10,22,134]{4,3,2,1,0:T(8,128)S(1)}, f32[2,2,10,22,134]{4,3,2,1,0:T(8,128)S(1)}, f32[2,2,10,22,134]{4,3,2,1,0:T(8,128)S(1)}) fusion(f32[2,2,10,24,136]{4,3,2,1,0:T(8,128)S(1)} %pad_maximum_fusion), kind=kLoop, calls=%fused_computation.169 | loop fusion | flops 707520 | bytes 6330240 | tf_op jit(solution)/shard_map/mul | solution.py:63
  65.2 0.5 fusion.101
  65.7 5.0 %fusion.103 = (f32[2,10,20,132]{3,2,1,0:T(8,128)S(1)}, f32[2,10,20,132]{3,2,1,0:T(8,128)}, f32[2,10,20,132]{3,2,1,0:T(8,128)}, f32[2,10,20,132]{3,2,1,0:T(8,128)...) fusion(f32[2,1,10,22,134]{4,3,2,1,0:T(8,128)S(1)} %fusion.101), kind=kLoop, calls=%fused_computation.200 | loop fusion | flops 580800 | bytes 4995840 | tf_op jit(solution)/shard_map/mul | solution.py:55
  70.8 2.6 %fusion.133 = (f32[2,10,20,132]{3,2,1,0:T(8,128)}, f32[2,10,20,132]{3,2,1,0:T(8,128)}, f32[2,10,20,132]{3,2,1,0:T(8,128)}, f32[2,10,20,132]{3,2,1,0:T(8,128)}, f...) fusion(f32[2,1,10,22,134]{4,3,2,1,0:T(8,128)S(1)} %fusion.101), kind=kLoop, calls=%fused_computation.240 | loop fusion | flops 158400 | bytes 3379200 | tf_op jit(solution)/shard_map/mul | solution.py:55
  73.3 1.0 slice_bitcast_fusion.1
  74.4 0.8 slice_bitcast_fusion.8
  75.1 0.3 broadcast_multiply_fusion.1
  75.5 0.3 copy-done.2
  75.8 0.0 copy-done.3
  75.8 0.0 copy-done.4
  75.8 0.0 copy-done.5
  75.8 8.9 %broadcast_multiply_fusion.2 = (f32[2,2,10,20,132]{4,3,2,1,0:T(8,128)S(1)}, f32[2,2,10,20,132]{4,3,2,1,0:T(8,128)S(1)}, f32[2,2,10,20,132]{4,3,2,1,0:T(8,128)S(1)}) fusion(f32[2,10,20,132]{3,2,1,0:T(8,128)} %get-tuple-element.53, f32[2,10,20,132]{3,2,1,0:T(8,128)S(1)} %multiply_add_fusion.1, f32[2,2,10,22,134]{4,3,2,1,0:T(8,128)S(1)} %get-tuple-element.21, ...), kind=kLoop, calls=%fused_computation.252 | loop fusion | flops 10032000 | bytes 17623040 | tf_op jit(solution)/shard_map/mul | solution.py:99
  84.7 0.0 copy-start.1
  84.8 5.9 %broadcast_multiply_fusion = (f32[2,2,10,18,130]{4,3,2,1,0:T(8,128)S(1)}, f32[2,2,10,18,130]{4,3,2,1,0:T(8,128)S(1)}) fusion(f32[2,10,18,130]{3,2,1,0:T(8,128)} %slice_bitcast_fusion.1, f32[2,10,18,130]{3,2,1,0:T(8,128)S(1)} %slice_bitcast_fusion, f32[2,2,10,20,132]{4,3,2,1,0:T(8,128)S(1)} %get-tuple-element.18, f32[2]{0:T(128)S(1)} %copy-done.5, ...), kind=kLoop, calls=%fused_computation.249 | loop fusion | flops 5335200 | bytes 12243008 | tf_op jit(solution)/shard_map/mul | solution.py:99
  90.6 1.8 %multiply_reduce_fusion.1 = (f32[2]{0:T(128)S(1)}, f32[2]{0:T(128)S(1)}, f32[2]{0:T(128)S(1)}, f32[2]{0:T(128)S(1)}) fusion(f32[2,2,10,20,132]{4,3,2,1,0:T(8,128)S(1)} %get-tuple-element.19, f32[2,2,10,18,130]{4,3,2,1,0:T(8,128)S(1)} %get-tuple-element.17, f32[2,10,16,128]{3,2,1,0:T(8,128)S(1)} %slice_bitcast_fusion.7, ...), kind=kLoop, calls=%fused_computation.313 | loop fusion | flops 5242872 | bytes 4917280 | tf_op jit(solution)/shard_map/reduce_sum | solution.py:87
  92.4 20.8 %all-reduce.5 = (f32[2]{0:T(128)S(1)}, f32[2]{0:T(128)S(1)}, f32[2]{0:T(128)S(1)}, f32[2]{0:T(128)S(1)}) all-reduce(f32[2]{0:T(128)S(1)} %get-tuple-element.23, f32[2]{0:T(128)S(1)} %get-tuple-element.6, f32[2]{0:T(128)S(1)} %get-tuple-element.7, ...), channel_id=1, replica_groups=mesh['group'=2,'plane'=4,'planey'=2,'ens'=2] {'plane','planey'}, use_global_device_ids=true, to_apply=%region_8.9 | all-reduce | flops 8 | bytes 64 | tf_op jit(solution)/shard_map/psum | solution.py:151
  113.3 0.3 fusion.184
  113.6 2.0 %all-gather = f32[4,10,16,128]{3,2,1,0:T(8,128)S(1)} all-gather(f32[2,10,16,128]{3,2,1,0:T(8,128)S(1)} %fusion.184), channel_id=2, replica_groups=mesh['group'=2,'plane'=4,'planey'=2,'ens'=2] {'ens'}, dimensions={0}, use_global_device_ids=true | all-gather | bytes 491520 | tf_op jit(solution)/shard_map/all_gather | solution.py:176
  115.6 0.7 broadcast_multiply_fusion.3
  (27 shorter events, 0.2 us)
Async XLA Ops:
  0.7 20.2 %collective-permute-start.4 = (f32[1,1,1,4,128]{4,3,2,1,0:T(4,128)S(1)}, f32[1,1,1,4,128]{4,3,2,1,0:T(4,128)S(1)}, u32[]{:S(2)}, u32[]{:S(2)}) collective-permute-start(f32[1,1,1,4,128]{4,3,2,1,0:T(4,128)S(1)} %get-tuple-element.72), channel_id=1, source_target_pairs={{0,4},{4,8},{8,12},{1,5},{5,9},{9,13},{2,6},{6,10},{10,14},{3,7},{... | collective-permute-start | bytes 6152 | tf_op jit(solution)/shard_map/ppermute | solution.py:19
  5.7 16.5 %collective-permute-start.5 = (f32[1,1,1,4,128]{4,3,2,1,0:T(4,128)S(1)}, f32[1,1,1,4,128]{4,3,2,1,0:T(4,128)S(1)}, u32[]{:S(2)}, u32[]{:S(2)}) collective-permute-start(f32[1,1,1,4,128]{4,3,2,1,0:T(4,128)S(1)} %get-tuple-element.73), channel_id=1, source_target_pairs={{4,0},{8,4},{12,8},{5,1},{9,5},{13,9},{6,2},{10,6},{14,10},{7,3},{... | collective-permute-start | bytes 6152 | tf_op jit(solution)/shard_map/ppermute | solution.py:21
  7.7 19.2 %collective-permute-start.8 = (f32[1,1,1,4,128]{4,3,2,1,0:T(4,128)S(1)}, f32[1,1,1,4,128]{4,3,2,1,0:T(4,128)S(1)}, u32[]{:S(2)}, u32[]{:S(2)}) collective-permute-start(f32[1,1,1,4,128]{4,3,2,1,0:T(4,128)S(1)} %get-tuple-element.70), channel_id=1, source_target_pairs={{0,4},{4,8},{8,12},{1,5},{5,9},{9,13},{2,6},{6,10},{10,14},{3,7},{... | collective-permute-start | bytes 6152 | tf_op jit(solution)/shard_map/ppermute | solution.py:19
  12.2 18.0 %collective-permute-start.9 = (f32[1,1,1,4,128]{4,3,2,1,0:T(4,128)S(1)}, f32[1,1,1,4,128]{4,3,2,1,0:T(4,128)S(1)}, u32[]{:S(2)}, u32[]{:S(2)}) collective-permute-start(f32[1,1,1,4,128]{4,3,2,1,0:T(4,128)S(1)} %get-tuple-element.71), channel_id=1, source_target_pairs={{4,0},{8,4},{12,8},{5,1},{9,5},{13,9},{6,2},{10,6},{14,10},{7,3},{... | collective-permute-start | bytes 6152 | tf_op jit(solution)/shard_map/ppermute | solution.py:21
  15.3 26.8 %collective-permute-start.12 = (f32[2,1,1,4,128]{4,3,0,2,1:T(4,128)S(1)}, f32[2,1,1,4,128]{4,3,0,2,1:T(4,128)S(1)}, u32[]{:S(2)}, u32[]{:S(2)}) collective-permute-start(f32[2,1,1,4,128]{4,3,0,2,1:T(4,128)S(1)} %get-tuple-element.64), channel_id=1, source_target_pairs={{0,4},{4,8},{8,12},{1,5},{5,9},{9,13},{2,6},{6,10},{10,14},{3,7},{... | collective-permute-start | bytes 12296 | tf_op jit(solution)/shard_map/ppermute | solution.py:19
  20.9 21.2 %collective-permute-start.13 = (f32[2,1,1,4,128]{4,3,0,2,1:T(4,128)S(1)}, f32[2,1,1,4,128]{4,3,0,2,1:T(4,128)S(1)}, u32[]{:S(2)}, u32[]{:S(2)}) collective-permute-start(f32[2,1,1,4,128]{4,3,0,2,1:T(4,128)S(1)} %get-tuple-element.65), channel_id=1, source_target_pairs={{4,0},{8,4},{12,8},{5,1},{9,5},{13,9},{6,2},{10,6},{14,10},{7,3},{... | collective-permute-start | bytes 12296 | tf_op jit(solution)/shard_map/ppermute | solution.py:21
  22.2 27.9 %collective-permute-start = (f32[2,2,10,4,128]{4,3,2,1,0:T(4,128)S(1)}, f32[2,2,10,4,128]{4,3,2,1,0:T(4,128)S(1)}, u32[]{:S(2)}, u32[]{:S(2)}) collective-permute-start(f32[2,2,10,4,128]{4,3,2,1,0:T(4,128)S(1)} %get-tuple-element.56), channel_id=1, source_target_pairs={{0,4},{4,8},{8,12},{1,5},{5,9},{9,13},{2,6},{6,10},{10,14},{3,7},{... | collective-permute-start | bytes 245768 | tf_op jit(solution)/shard_map/ppermute | solution.py:19
  26.9 4.8 %collective-permute-start.6 = (f32[1,1,1,24,4]{4,3,2,1,0:T(8,128)S(1)}, f32[1,1,1,24,4]{4,3,2,1,0:T(8,128)S(1)}, u32[]{:S(2)}, u32[]{:S(2)}) collective-permute-start(f32[1,1,1,24,4]{4,3,2,1,0:T(8,128)S(1)} %get-tuple-element.68), channel_id=1, source_target_pairs={{0,2},{1,3},{4,6},{5,7},{8,10},{9,11},{12,14},{13,15},{16,18},{17,... | collective-permute-start | bytes 1160 | tf_op jit(solution)/shard_map/ppermute | solution.py:19
  30.3 5.9 %collective-permute-start.7 = (f32[1,1,1,24,4]{4,3,2,1,0:T(8,128)S(1)}, f32[1,1,1,24,4]{4,3,2,1,0:T(8,128)S(1)}, u32[]{:S(2)}, u32[]{:S(2)}) collective-permute-start(f32[1,1,1,24,4]{4,3,2,1,0:T(8,128)S(1)} %get-tuple-element.69), channel_id=1, source_target_pairs={{2,0},{3,1},{6,4},{7,5},{10,8},{11,9},{14,12},{15,13},{18,16},{19,... | collective-permute-start | bytes 1160 | tf_op jit(solution)/shard_map/ppermute | solution.py:21
  31.7 5.9 %collective-permute-start.10 = (f32[1,1,1,24,4]{4,3,2,1,0:T(8,128)S(1)}, f32[1,1,1,24,4]{4,3,2,1,0:T(8,128)S(1)}, u32[]{:S(2)}, u32[]{:S(2)}) collective-permute-start(f32[1,1,1,24,4]{4,3,2,1,0:T(8,128)S(1)} %get-tuple-element.66), channel_id=1, source_target_pairs={{0,2},{1,3},{4,6},{5,7},{8,10},{9,11},{12,14},{13,15},{16,18},{17,... | collective-permute-start | bytes 1160 | tf_op jit(solution)/shard_map/ppermute | solution.py:19
  36.2 5.6 %collective-permute-start.11 = (f32[1,1,1,24,4]{4,3,2,1,0:T(8,128)S(1)}, f32[1,1,1,24,4]{4,3,2,1,0:T(8,128)S(1)}, u32[]{:S(2)}, u32[]{:S(2)}) collective-permute-start(f32[1,1,1,24,4]{4,3,2,1,0:T(8,128)S(1)} %get-tuple-element.67), channel_id=1, source_target_pairs={{2,0},{3,1},{6,4},{7,5},{10,8},{11,9},{14,12},{15,13},{18,16},{19,... | collective-permute-start | bytes 1160 | tf_op jit(solution)/shard_map/ppermute | solution.py:21
  37.6 12.5 %collective-permute-start.1 = (f32[2,2,10,4,128]{4,3,2,1,0:T(4,128)S(1)}, f32[2,2,10,4,128]{4,3,2,1,0:T(4,128)S(1)}, u32[]{:S(2)}, u32[]{:S(2)}) collective-permute-start(f32[2,2,10,4,128]{4,3,2,1,0:T(4,128)S(1)} %get-tuple-element.57), channel_id=1, source_target_pairs={{4,0},{8,4},{12,8},{5,1},{9,5},{13,9},{6,2},{10,6},{14,10},{7,3},{... | collective-permute-start | bytes 245768 | tf_op jit(solution)/shard_map/ppermute | solution.py:21
  42.2 3.2 %collective-permute-start.14 = (f32[2,1,1,24,4]{4,3,0,2,1:T(8,128)S(1)}, f32[2,1,1,24,4]{4,3,0,2,1:T(8,128)S(1)}, u32[]{:S(2)}, u32[]{:S(2)}) collective-permute-start(f32[2,1,1,24,4]{4,3,0,2,1:T(8,128)S(1)} %get-tuple-element.62), channel_id=1, source_target_pairs={{0,2},{1,3},{4,6},{5,7},{8,10},{9,11},{12,14},{13,15},{16,18},{17,... | collective-permute-start | bytes 2312 | tf_op jit(solution)/shard_map/ppermute | solution.py:19
  43.8 5.7 %collective-permute-start.15 = (f32[2,1,1,24,4]{4,3,0,2,1:T(8,128)S(1)}, f32[2,1,1,24,4]{4,3,0,2,1:T(8,128)S(1)}, u32[]{:S(2)}, u32[]{:S(2)}) collective-permute-start(f32[2,1,1,24,4]{4,3,0,2,1:T(8,128)S(1)} %get-tuple-element.63), channel_id=1, source_target_pairs={{2,0},{3,1},{6,4},{7,5},{10,8},{11,9},{14,12},{15,13},{18,16},{19,... | collective-permute-start | bytes 2312 | tf_op jit(solution)/shard_map/ppermute | solution.py:21
  49.7 1.0 copy-start
  50.9 8.0 %collective-permute-start.2 = (f32[2,2,10,24,4]{4,3,2,1,0:T(8,128)S(1)}, f32[2,2,10,24,4]{4,3,2,1,0:T(8,128)S(1)}, u32[]{:S(2)}, u32[]{:S(2)}) collective-permute-start(f32[2,2,10,24,4]{4,3,2,1,0:T(8,128)S(1)} %get-tuple-element.54), channel_id=1, source_target_pairs={{0,2},{1,3},{4,6},{5,7},{8,10},{9,11},{12,14},{13,15},{16,18},{17,... | collective-permute-start | bytes 46088 | tf_op jit(solution)/shard_map/ppermute | solution.py:19
  52.6 10.7 %collective-permute-start.3 = (f32[2,2,10,24,4]{4,3,2,1,0:T(8,128)S(1)}, f32[2,2,10,24,4]{4,3,2,1,0:T(8,128)S(1)}, u32[]{:S(2)}, u32[]{:S(2)}) collective-permute-start(f32[2,2,10,24,4]{4,3,2,1,0:T(8,128)S(1)} %get-tuple-element.55), channel_id=1, source_target_pairs={{2,0},{3,1},{6,4},{7,5},{10,8},{11,9},{14,12},{15,13},{18,16},{19,... | collective-permute-start | bytes 46088 | tf_op jit(solution)/shard_map/ppermute | solution.py:21
  75.1 0.7 copy-start.2
  75.1 0.7 copy-start.3
  75.1 0.7 copy-start.4
  75.1 0.7 copy-start.5
  84.7 5.9 %copy-start.1 = (f32[2,10,16,128]{3,2,1,0:T(8,128)S(1)}, f32[2,10,16,128]{3,2,1,0:T(8,128)}, u32[]{:S(2)}) copy-start(f32[2,10,16,128]{3,2,1,0:T(8,128)} %slice_bitcast_fusion.8) | copy-start | bytes 491524
